TPU v7x, 32 devices: a whole 2x2x4 slice. The times are simulated.
32 devices in a mesh: grp: 4 (over y, x), dev: 8 (over z, core).
Axes of the slice: x: 2, y: 2, z: 4, core: 2. Of those that a mesh axis runs over, the one named last changes fastest.
Arguments:
- table: bfloat16 [8, 32768, 256], P('grp', 'dev'), may hold values from -0.75 to 0.75
- token_ids: int32 [8192], P(('grp', 'dev')), may hold values from 0 to 32767, as said below
- hidden: bfloat16 [8192, 2560], P(('grp', 'dev')), may hold values from -6 to 6
- w_proj: bfloat16 [2560, 2048], replicated, may hold values from -0.125 to 0.125
- norm_gain: float32 [256], replicated, may hold values from 0.5 to 1.5
Outputs:
- served_table: bfloat16 [8, 4, 1024, 2048], P('dev', 'grp')
- layer_inputs: bfloat16 [8192, 8, 256], P(('grp', 'dev'))
Inputs may be any that keep to these rules, and one draw needn't show every extreme that they name: `token_ids`: of the 256 tokens of one device, at most 16 have ids in any one aligned block of 1024 vocabulary rows, and exactly 16 in some block.
All inputs are finite; a program needn't handle non-finite values.
Results may differ from a plain program's by a relative error of at most 0.001.
Values may be sent and summed in bfloat16 or wider, within the bound.
A program may use at most 128 MiB of HBM per device.

v0:
```python
import math
import jax
import jax.numpy as jnp
from jax import lax
from jax.sharding import PartitionSpec as P


def lookup(all_ids, local_rows, base):
    owned = local_rows.shape[0]
    count = all_ids.shape[0]
    block = math.gcd(count, 512)
    blocks = all_ids.reshape(count // block, block)

    def one_block(ids_block):
        onehot = (ids_block[:, None] - base == jnp.arange(owned, dtype=jnp.int32)[None, :]).astype(
            jnp.bfloat16
        )
        return jnp.dot(onehot, local_rows, preferred_element_type=jnp.float32).astype(jnp.bfloat16)

    return lax.map(one_block, blocks).reshape(count, local_rows.shape[1])


def on_device(table, token_ids, hidden, w_proj, norm_gain):
    n_grp = lax.axis_size("grp")
    n_dev = lax.axis_size("dev")
    g_index = lax.axis_index("grp")
    d_index = lax.axis_index("dev")
    layer_share, vocab_share, width = table.shape
    layers = layer_share * n_grp
    tok_count = token_ids.shape[0]
    moved = lax.all_to_all(table, "grp", split_axis=1, concat_axis=0, tiled=True)
    row_count = moved.shape[1]
    served_rows = jnp.transpose(moved, (1, 0, 2)).reshape(row_count, layers * width)
    served_table = served_rows.reshape(1, 1, row_count, layers * width)
    peers = n_grp * n_dev
    capacity = max(2, 2 * tok_count // peers)
    owner_block = token_ids // row_count
    owner_peer = owner_block % n_grp * n_dev + owner_block // n_grp
    positions = jnp.arange(tok_count, dtype=jnp.int32)
    same_peer = owner_peer[:, None] == owner_peer[None, :]
    earlier = positions[None, :] < positions[:, None]
    slot_index = jnp.sum((same_peer & earlier).astype(jnp.int32), axis=1)
    wanted = owner_peer * capacity + slot_index
    slot_hit = (wanted[:, None] == jnp.arange(peers * capacity, dtype=jnp.int32)[None, :]).astype(
        jnp.int32
    )
    outgoing = jnp.sum(slot_hit * (token_ids + 1)[:, None], axis=0) - 1
    base = (d_index * n_grp + g_index) * row_count
    incoming = lax.all_to_all(
        outgoing.reshape(peers, capacity), ("grp", "dev"), split_axis=0, concat_axis=0, tiled=True
    )
    found = lookup(incoming.reshape(peers * capacity), served_rows, base)
    found = found.reshape(peers, capacity, layers * width)
    replies = lax.all_to_all(found, ("grp", "dev"), split_axis=0, concat_axis=0, tiled=True)
    picker = slot_hit.astype(jnp.bfloat16)
    emb = jnp.dot(
        picker,
        replies.reshape(peers * capacity, layers * width),
        preferred_element_type=jnp.float32,
    )
    proj = jnp.dot(hidden, w_proj, preferred_element_type=jnp.float32).reshape(
        tok_count, layers, width
    )
    mean_sq = jnp.mean(proj * proj, axis=-1, keepdims=True)
    normed = proj / jnp.sqrt(mean_sq + 1e-06) * norm_gain
    emb = emb.reshape(tok_count, layers, width)
    layer_inputs = ((normed + math.sqrt(width) * emb) / math.sqrt(2.0)).astype(jnp.bfloat16)
    return (served_table, layer_inputs)


def solution(mesh):
    in_specs = (P("grp", "dev", None), P(("grp", "dev")), P(("grp", "dev"), None), P(), P())
    out_specs = (P("dev", "grp", None, None), P(("grp", "dev"), None, None))
    return jax.shard_map(
        on_device, mesh=mesh, in_specs=in_specs, out_specs=out_specs, check_vma=False
    )
```

profile of v0, /device:TPU:0, one launch (start us, length us, event | category | flops | bytes accessed | tf_op | source)
XLA Modules:
  0.0 152.2 jit_solution(1475072987152448503)
XLA Ops:
  0.6 0.0 copy-start
  0.6 0.8 fusion.10
  1.4 0.2 convert_reduce_fusion
  1.6 0.2 select_reduce_fusion
  1.8 0.7 sub.35
  2.5 7.3 %all-to-all-start.1 = ((s32[32,1,16]{2,1,0:T(1,128)}), s32[32,1,16]{2,1,0:T(1,128)S(1)}, u32[]{:S(2)}, u32[]{:S(2)}) async-start(s32[32,1,16]{2,1,0:T(1,128)} %bitcast.6), calls=%async_computation.1 | async-start | bytes 32768 | tf_op jit(solution)/shard_map/all_to_all | solution.py:49
  9.8 10.1 %copy.49 = bf16[2,4096,256]{2,0,1:T(2,128)(2,1)} copy(bf16[2,4096,256]{2,1,0:T(8,128)(2,1)} %param.5) | data formatting | bytes 8388608 | tf_op args[0]
  19.9 0.0 all-to-all-done.1
  19.9 4.9 %all-to-all-start = ((bf16[2,4096,256]{2,0,1:T(2,128)(2,1)}), bf16[2,4096,256]{2,0,1:T(2,128)(2,1)}, u32[]{:S(2)}, u32[]{:S(2)}) async-start(bf16[2,4096,256]{2,0,1:T(2,128)(2,1)} %copy.49), calls=%async_computation | async-start | bytes 8388608 | tf_op jit(solution)/shard_map/all_to_all | solution.py:31
  24.9 0.1 sub.38
  24.9 48.0 %all-to-all-done = bf16[2,4096,256]{2,0,1:T(2,128)(2,1)} async-done(((bf16[2,4096,256]{2,0,1:T(2,128)(2,1)}), bf16[2,4096,256]{2,0,1:T(2,128)(2,1)}, u32[]{:S(2)}, u32[]{:S(2)}) %all-to-all-start) | async-done | bytes 4194336 | tf_op jit(solution)/shard_map/all_to_all | solution.py:31
  72.9 2.7 %copy.50 = bf16[2,4096,256]{2,1,0:T(8,128)(2,1)S(1)} copy(bf16[2,4096,256]{2,0,1:T(2,128)(2,1)} %all-to-all-done) | data formatting | bytes 8388608 | tf_op jit(solution)/shard_map/all_to_all | solution.py:31
  75.6 2.3 %copy.51 = bf16[4,2,1024,256]{3,2,1,0:T(8,128)(2,1)} copy(bf16[4,2,1024,256]{3,2,0,1:T(8,128)(2,1)S(1)} %bitcast.36) | data formatting | bytes 8388608 | tf_op jit(solution)/shard_map/all_to_all | solution.py:31
  77.9 6.4 %copy.52 = bf16[1024,8,256]{0,2,1:T(8,128)(2,1)} copy(bf16[1024,8,256]{2,0,1:T(8,128)(2,1)} %bitcast.37) | data formatting | bytes 8388608 | tf_op jit(solution)/shard_map/transpose | solution.py:33
  84.4 5.9 %convolution_convert_fusion = bf16[512,2048]{1,0:T(8,128)(2,1)} fusion(bf16[1024,2048]{0,1:T(8,128)(2,1)} %bitcast.34, s32[512]{0:T(512)S(1)} %sub.38), kind=kOutput, calls=%fused_computation | convolution fusion | flops 2149056512 | bytes 6293504 | tf_op jit(solution)/shard_map/while/body/eval_jaxpr/dot_general | solution.py:18
  90.3 4.8 %all-to-all-start.2 = ((bf16[32,16,2048]{2,1,0:T(8,128)(2,1)}), bf16[32,16,2048]{2,1,0:T(8,128)(2,1)S(1)}, u32[]{:S(2)}, u32[]{:S(2)}) async-start(bf16[32,16,2048]{2,1,0:T(8,128)(2,1)} %bitcast.42), calls=%async_computation.2 | async-start | bytes 4194304 | tf_op jit(solution)/shard_map/all_to_all | solution.py:54
  95.1 0.0 copy-done
  95.1 5.6 %fusion.11 = f32[256,2048]{1,0:T(8,128)S(1)} fusion(bf16[256,2560]{1,0:T(8,128)(2,1)S(1)} %copy-done, bf16[2560,2048]{1,0:T(8,128)(2,1)} %param.8), kind=kOutput, calls=%fused_computation.33 | convolution fusion | flops 2684354560 | bytes 13893632 | tf_op jit(solution)/shard_map/dot_general | solution.py:61
  100.7 0.0 copy-start.1
  100.7 0.9 copy.61
  101.6 0.5 copy-done.1
  102.1 0.3 multiply_reduce_fusion
  102.4 0.1 copy.53
  102.5 6.4 %copy.58 = bf16[1,1,1024,2048]{3,2,1,0:T(8,128)(2,1)} copy(bf16[1,1,1024,2048]{2,3,1,0:T(8,128)(2,1)} %bitcast.35) | data formatting | bytes 8388608
  108.9 36.2 %all-to-all-done.2 = bf16[32,16,2048]{2,1,0:T(8,128)(2,1)S(1)} async-done(((bf16[32,16,2048]{2,1,0:T(8,128)(2,1)}), bf16[32,16,2048]{2,1,0:T(8,128)(2,1)S(1)}, u32[]{:S(2)}, u32[]{:S(2)}) %all-to-all-start.2) | async-done | bytes 2097184 | tf_op jit(solution)/shard_map/all_to_all | solution.py:54
  145.1 0.0 copy-start.2
  145.1 2.5 %copy.57 = bf16[512,2048]{0,1:T(8,128)(2,1)} copy(bf16[512,2048]{1,0:T(8,128)(2,1)S(1)} %bitcast.38) | data formatting | bytes 4194304 | tf_op jit(solution)/shard_map/reshape | solution.py:58
  147.6 0.0 copy-done.2
  147.6 3.0 %fusion.3 = bf16[256,8,256]{2,0,1:T(8,128)(2,1)S(1)} fusion(f32[32,8,8,256]{3,2,1,0:T(8,128)} %bitcast.41, bf16[8,256,512]{2,1,0:T(8,128)(2,1)} %bitcast.43, f32[256]{0:T(256)S(1)} %copy-done.2, f32[256,8]{0,1:T(8,128)S(1)} %add_sqrt_fusion, s32[256]{0:T(256)S(1)} %multiply_add_fusion), kind=kOutput, calls=%fused_computation.7 | convolution fusion | flops 540409856 | bytes 5253120 | tf_op jit(solution)/shard_map/dot_general | solution.py:56
  150.6 1.6 %copy.59 = bf16[256,8,256]{2,1,0:T(8,128)(2,1)} copy(bf16[256,8,256]{2,0,1:T(8,128)(2,1)S(1)} %fusion.3) | data formatting | bytes 2097152
  (4 shorter events, 0.1 us)
Async XLA Ops:
  0.6 94.4 %copy-start = (bf16[256,2560]{1,0:T(8,128)(2,1)S(1)}, bf16[256,2560]{1,0:T(8,128)(2,1)}, u32[]{:S(2)}) copy-start(bf16[256,2560]{1,0:T(8,128)(2,1)} %param.7) | copy-start | bytes 3932164
  2.5 17.4 %all-to-all-start.1 = ((s32[32,1,16]{2,1,0:T(1,128)}), s32[32,1,16]{2,1,0:T(1,128)S(1)}, u32[]{:S(2)}, u32[]{:S(2)}) async-start(s32[32,1,16]{2,1,0:T(1,128)} %bitcast.6), calls=%async_computation.1 | async-start | bytes 32768 | tf_op jit(solution)/shard_map/all_to_all | solution.py:49
  19.9 53.0 %all-to-all-start = ((bf16[2,4096,256]{2,0,1:T(2,128)(2,1)}), bf16[2,4096,256]{2,0,1:T(2,128)(2,1)}, u32[]{:S(2)}, u32[]{:S(2)}) async-start(bf16[2,4096,256]{2,0,1:T(2,128)(2,1)} %copy.49), calls=%async_computation | async-start | bytes 8388608 | tf_op jit(solution)/shard_map/all_to_all | solution.py:31
  90.3 54.8 %all-to-all-start.2 = ((bf16[32,16,2048]{2,1,0:T(8,128)(2,1)}), bf16[32,16,2048]{2,1,0:T(8,128)(2,1)S(1)}, u32[]{:S(2)}, u32[]{:S(2)}) async-start(bf16[32,16,2048]{2,1,0:T(8,128)(2,1)} %bitcast.42), calls=%async_computation.2 | async-start | bytes 4194304 | tf_op jit(solution)/shard_map/all_to_all | solution.py:54
  100.7 1.4 copy-start.1
  145.1 2.5 %copy-start.2 = (f32[256]{0:T(256)S(1)}, f32[256]{0:T(256)}, u32[]{:S(2)}) copy-start(f32[256]{0:T(256)} %param.9) | copy-start | bytes 3076
where the time goes:
time: 153 us; the launch traced here: 152 us
  waiting for transfers between devices  84.1 us (55%)
  local copies, waits for them, and re-layouts  34.3 us (22%)
  starting transfers between devices  16.9 us (11%)
  matrix products  14.5 us (9%)
  other arithmetic  1.55 us (1%)
    all_to_all x1, waiting for transfers between devices, on_device(): lax.all_to_all(table, 'grp', split_axis=1, concat_axis=0, tiled=True)  48 us
    all_to_all x1, waiting for transfers between devices, on_device(): lax.all_to_all(found, ('grp', 'dev'), split_axis=0, concat_axis=0, tiled=...  36.2 us
    unnamed x10, local copies, waits for them, and re-layouts  19.5 us
    all_to_all x1, starting transfers between devices, on_device(): lax.all_to_all(outgoing.reshape(peers, capacity), ('grp', 'dev'), split_a...  7.33 us
    transpose x1, local copies, waits for them, and re-layouts, on_device(): jnp.transpose(moved, (1, 0, 2)).reshape(row_count, layers * width)  6.44 us
    dot_general x1, matrix products, one_block(): jnp.dot(onehot, local_rows, preferred_element_type=jnp.float32)  5.91 us
    dot_general x1, matrix products, on_device(): jnp.dot(hidden, w_proj, preferred_element_type=jnp.float32)  5.61 us
    all_to_all x2, local copies, waits for them, and re-layouts, on_device(): lax.all_to_all(table, 'grp', split_axis=1, concat_axis=0, tiled=True)  5.05 us
  transfers between devices with their start and end apart: 3, of which 2 were waited for; matrix products, arithmetic and copies ran while one was open for 15% of the time, Pallas kernels for 0%

commit v1 on v0

--- a/solution.py
+++ b/solution.py
@@ -28,7 +28,10 @@
     layer_share, vocab_share, width = table.shape
     layers = layer_share * n_grp
     tok_count = token_ids.shape[0]
-    moved = lax.all_to_all(table, "grp", split_axis=1, concat_axis=0, tiled=True)
+    moved = jnp.concatenate(
+        lax.all_to_all(jnp.stack(jnp.split(table, lax.axis_size("grp"), axis=1)), "grp", 0, 0),
+        axis=0,
+    )
     row_count = moved.shape[1]
     served_rows = jnp.transpose(moved, (1, 0, 2)).reshape(row_count, layers * width)
     served_table = served_rows.reshape(1, 1, row_count, layers * width)

time: 153 us -> 136 us (0.89)
  local copies, waits for them, and re-layouts: 34.3 us -> 25.4 us
  waiting for transfers between devices: 84.1 us -> 78.6 us
  other arithmetic: 1.55 us -> 3.85 us
  matrix products: 14.5 us -> 12.4 us
  starting transfers between devices: 16.9 us -> 15 us
    unnamed x10 -> x9, local copies, waits for them, and re-layouts: 19.5 us -> 5.7 us
    another operation x0 -> x2, local copies, waits for them, and re-layouts: none -> 9.82 us  [the longest x1 7.37 us: on_device(): served_table = served_rows.reshape(1, 1, row_count, layers * width)]
    all_to_all x1, waiting for transfers between devices: 36.2 us -> 28.7 us  [on_device(): lax.all_to_all(found, ('grp', 'dev'), split_axis=0, concat_axis=0, tiled=...]
    reshape x0 -> x1, local copies, waits for them, and re-layouts: none -> 6.55 us  [on_device(): jnp.concatenate(lax.all_to_all(jnp.stack(jnp.split(table, lax.axis_size('...]
    transpose x1 -> x0, local copies, waits for them, and re-layouts: 6.44 us -> none  [on_device(): jnp.transpose(moved, (1, 0, 2)).reshape(row_count, layers * width)]
    all_to_all x2 -> x0, local copies, waits for them, and re-layouts: 5.05 us -> none  [on_device(): lax.all_to_all(table, 'grp', split_axis=1, concat_axis=0, tiled=True)]
    all_to_all x1, waiting for transfers between devices: 0.01 us -> 2.34 us  [on_device(): lax.all_to_all(outgoing.reshape(peers, capacity), ('grp', 'dev'), split_a...]
    another operation x0 -> x1, other arithmetic: none -> 2.29 us  [on_device(): jnp.stack(jnp.split(table, lax.axis_size('grp'), axis=1))]
  transfers between devices with their start and end apart: 3 -> 3, of which waited for: 2 -> 3; matrix products, arithmetic and copies ran while one was open for 15% -> 19% of each run, Pallas kernels for 0% -> 0%
where the time goes in v1:
time: 136 us
  waiting for transfers between devices  78.6 us (58%)
  local copies, waits for them, and re-layouts  25.4 us (19%)
  starting transfers between devices  15 us (11%)
  matrix products  12.4 us (9%)
  other arithmetic  3.85 us (3%)
    all_to_all x1, waiting for transfers between devices, on_device(): lax.all_to_all(jnp.stack(jnp.split(table, lax.axis_size('grp'), axis=1)),...  47.6 us
    all_to_all x1, waiting for transfers between devices, on_device(): lax.all_to_all(found, ('grp', 'dev'), split_axis=0, concat_axis=0, tiled=...  28.7 us
    another operation x1, local copies, waits for them, and re-layouts, on_device(): served_table = served_rows.reshape(1, 1, row_count, layers * width)  7.37 us
    all_to_all x1, starting transfers between devices, on_device(): lax.all_to_all(outgoing.reshape(peers, capacity), ('grp', 'dev'), split_a...  7.33 us
    reshape x1, local copies, waits for them, and re-layouts, on_device(): jnp.concatenate(lax.all_to_all(jnp.stack(jnp.split(table, lax.axis_size('...  6.55 us
    unnamed x9, local copies, waits for them, and re-layouts  5.7 us
    dot_general x1, matrix products, on_device(): jnp.dot(hidden, w_proj, preferred_element_type=jnp.float32)  5.61 us
    all_to_all x1, starting transfers between devices, on_device(): lax.all_to_all(jnp.stack(jnp.split(table, lax.axis_size('grp'), axis=1)),...  4.86 us
  transfers between devices with their start and end apart: 3, of which 3 were waited for; matrix products, arithmetic and copies ran while one was open for 19% of the time, Pallas kernels for 0%

profile of v1, /device:TPU:0, one launch (start us, length us, event | category | flops | bytes accessed | tf_op | source)
XLA Modules:
  0.0 135.9 jit_solution(8997673052443607289)
XLA Ops:
  0.6 0.0 copy-start
  0.6 0.8 fusion.10
  1.4 0.2 convert_reduce_fusion
  1.6 0.2 select_reduce_fusion
  1.8 0.7 sub.35
  2.5 7.3 %all-to-all-start.1 = ((s32[32,1,16]{2,1,0:T(1,128)}), s32[32,1,16]{2,1,0:T(1,128)S(1)}, u32[]{:S(2)}, u32[]{:S(2)}) async-start(s32[32,1,16]{2,1,0:T(1,128)} %bitcast.7), calls=%async_computation.1 | async-start | bytes 32768 | tf_op jit(solution)/shard_map/all_to_all | solution.py:52
  9.8 2.5 %slice_bitcast_fusion.3 = (bf16[1,2,1024,256]{3,2,1,0:T(8,128)(2,1)S(1)}, bf16[1,2,1024,256]{3,2,1,0:T(8,128)(2,1)S(1)}, bf16[1,2,1024,256]{3,2,1,0:T(8,128)(2,1)S(1)}, bf16[1,2,1024,256]{3,2,1,0:T(8,128)(2,1)S(1)}) fusion(bf16[2,4096,256]{2,1,0:T(8,128)(2,1)} %param.5), kind=kLoop, calls=%fused_computation.13 | loop fusion | bytes 8388608 | tf_op jit(solution)/shard_map/stack | solution.py:32
  12.3 2.3 %pad_maximum_fusion = bf16[4,2,1024,256]{3,2,1,0:T(8,128)(2,1)} fusion(bf16[1,2,1024,256]{3,2,1,0:T(8,128)(2,1)S(1)} %get-tuple-element.29, bf16[1,2,1024,256]{3,2,1,0:T(8,128)(2,1)S(1)} %get-tuple-element.30, bf16[1,2,1024,256]{3,2,1,0:T(8,128)(2,1)S(1)} %get-tuple-element.28, bf16[1,2,1024,256]{3,2,1,0:T(8,128)(2,1)S(1)} %get-tuple-element.27), kind=kLoop, calls=%fused_computation | loop fusion | flops 6291456 | bytes 8388608 | tf_op jit(solution)/shard_map/stack | solution.py:32
  14.6 2.3 %all-to-all-done.1 = s32[32,1,16]{2,1,0:T(1,128)S(1)} async-done(((s32[32,1,16]{2,1,0:T(1,128)}), s32[32,1,16]{2,1,0:T(1,128)S(1)}, u32[]{:S(2)}, u32[]{:S(2)}) %all-to-all-start.1) | async-done | bytes 2080 | tf_op jit(solution)/shard_map/all_to_all | solution.py:52
  16.9 4.9 %all-to-all-start = ((bf16[4,2,1024,256]{3,2,1,0:T(8,128)(2,1)}), bf16[4,2,1024,256]{3,2,1,0:T(8,128)(2,1)}, u32[]{:S(2)}, u32[]{:S(2)}) async-start(bf16[4,2,1024,256]{3,2,1,0:T(8,128)(2,1)} %pad_maximum_fusion), calls=%async_computation | async-start | bytes 8388608 | tf_op jit(solution)/shard_map/all_to_all | solution.py:32
  21.9 0.1 sub.38
  21.9 47.6 %all-to-all-done = bf16[4,2,1024,256]{3,2,1,0:T(8,128)(2,1)} async-done(((bf16[4,2,1024,256]{3,2,1,0:T(8,128)(2,1)}), bf16[4,2,1024,256]{3,2,1,0:T(8,128)(2,1)}, u32[]{:S(2)}, u32[]{:S(2)}) %all-to-all-start) | async-done | bytes 4194336 | tf_op jit(solution)/shard_map/all_to_all | solution.py:32
  69.5 2.8 %copy.35 = bf16[128,8,8,256]{3,1,2,0:T(8,128)(2,1)S(1)} copy(bf16[128,8,8,256]{3,1,0,2:T(8,128)(2,1)} %bitcast.35) | data formatting | bytes 8388608
  72.3 3.7 %convolution_convert_fusion = bf16[512,2048]{1,0:T(8,128)(2,1)} fusion(bf16[1024,2048]{1,0:T(8,128)(2,1)S(1)} %bitcast.45, s32[512]{0:T(512)S(1)} %sub.38), kind=kOutput, calls=%fused_computation.1 | convolution fusion | flops 2149056512 | bytes 6293504 | tf_op jit(solution)/shard_map/while/body/eval_jaxpr/dot_general | solution.py:18
  76.0 2.8 %all-to-all-start.2 = ((bf16[32,16,2048]{2,1,0:T(8,128)(2,1)}), bf16[32,16,2048]{2,1,0:T(8,128)(2,1)S(1)}, u32[]{:S(2)}, u32[]{:S(2)}) async-start(bf16[32,16,2048]{2,1,0:T(8,128)(2,1)} %bitcast.48), calls=%async_computation.2 | async-start | bytes 4194304 | tf_op jit(solution)/shard_map/all_to_all | solution.py:57
  78.8 0.0 copy-done
  78.8 5.6 %fusion.11 = f32[256,2048]{1,0:T(8,128)S(1)} fusion(bf16[256,2560]{1,0:T(8,128)(2,1)S(1)} %copy-done, bf16[2560,2048]{1,0:T(8,128)(2,1)} %param.8), kind=kOutput, calls=%fused_computation.39 | convolution fusion | flops 2684354560 | bytes 13893632 | tf_op jit(solution)/shard_map/dot_general | solution.py:64
  84.4 0.0 copy-start.1
  84.5 0.9 copy.34
  85.3 0.5 copy-done.1
  85.8 0.3 multiply_reduce_fusion
  86.2 0.1 copy.28
  86.3 6.5 %copy.41 = bf16[8,1024,256]{2,0,1:T(8,128)(2,1)} copy(bf16[8,1024,256]{2,1,0:T(8,128)(2,1)} %bitcast.4) | data formatting | bytes 8388608 | tf_op jit(solution)/shard_map/reshape | solution.py:31
  92.8 7.4 %reshape_reshape.7 = bf16[1,1,1024,2048]{3,2,1,0:T(8,128)(2,1)} reshape(bf16[1024,8,256]{2,1,0:T(8,128)(2,1)} %bitcast.42) | data formatting | bytes 8388608 | tf_op jit(solution)/shard_map/reshape;reshape | solution.py:37
  100.2 28.7 %all-to-all-done.2 = bf16[32,16,2048]{2,1,0:T(8,128)(2,1)S(1)} async-done(((bf16[32,16,2048]{2,1,0:T(8,128)(2,1)}), bf16[32,16,2048]{2,1,0:T(8,128)(2,1)S(1)}, u32[]{:S(2)}, u32[]{:S(2)}) %all-to-all-start.2) | async-done | bytes 2097184 | tf_op jit(solution)/shard_map/all_to_all | solution.py:57
  128.8 0.0 copy-start.2
  128.9 2.5 %copy.31 = bf16[512,2048]{0,1:T(8,128)(2,1)} copy(bf16[512,2048]{1,0:T(8,128)(2,1)S(1)} %bitcast.43) | data formatting | bytes 4194304 | tf_op jit(solution)/shard_map/reshape | solution.py:61
  131.4 0.0 copy-done.2
  131.4 3.0 %fusion.3 = bf16[256,8,256]{2,0,1:T(8,128)(2,1)S(1)} fusion(f32[32,8,8,256]{3,2,1,0:T(8,128)} %bitcast.47, bf16[8,256,512]{2,1,0:T(8,128)(2,1)} %bitcast.49, f32[256]{0:T(256)S(1)} %copy-done.2, f32[256,8]{0,1:T(8,128)S(1)} %add_sqrt_fusion, s32[256]{0:T(256)S(1)} %multiply_add_fusion), kind=kOutput, calls=%fused_computation.8 | convolution fusion | flops 540409856 | bytes 5253120 | tf_op jit(solution)/shard_map/dot_general | solution.py:59
  134.4 1.6 %copy.32 = bf16[256,8,256]{2,1,0:T(8,128)(2,1)} copy(bf16[256,8,256]{2,0,1:T(8,128)(2,1)S(1)} %fusion.3) | data formatting | bytes 2097152
  (4 shorter events, 0.1 us)
Async XLA Ops:
  0.6 78.2 %copy-start = (bf16[256,2560]{1,0:T(8,128)(2,1)S(1)}, bf16[256,2560]{1,0:T(8,128)(2,1)}, u32[]{:S(2)}) copy-start(bf16[256,2560]{1,0:T(8,128)(2,1)} %param.7) | copy-start | bytes 3932164
  2.5 14.4 %all-to-all-start.1 = ((s32[32,1,16]{2,1,0:T(1,128)}), s32[32,1,16]{2,1,0:T(1,128)S(1)}, u32[]{:S(2)}, u32[]{:S(2)}) async-start(s32[32,1,16]{2,1,0:T(1,128)} %bitcast.7), calls=%async_computation.1 | async-start | bytes 32768 | tf_op jit(solution)/shard_map/all_to_all | solution.py:52
  16.9 52.6 %all-to-all-start = ((bf16[4,2,1024,256]{3,2,1,0:T(8,128)(2,1)}), bf16[4,2,1024,256]{3,2,1,0:T(8,128)(2,1)}, u32[]{:S(2)}, u32[]{:S(2)}) async-start(bf16[4,2,1024,256]{3,2,1,0:T(8,128)(2,1)} %pad_maximum_fusion), calls=%async_computation | async-start | bytes 8388608 | tf_op jit(solution)/shard_map/all_to_all | solution.py:32
  76.0 52.8 %all-to-all-start.2 = ((bf16[32,16,2048]{2,1,0:T(8,128)(2,1)}), bf16[32,16,2048]{2,1,0:T(8,128)(2,1)S(1)}, u32[]{:S(2)}, u32[]{:S(2)}) async-start(bf16[32,16,2048]{2,1,0:T(8,128)(2,1)} %bitcast.48), calls=%async_computation.2 | async-start | bytes 4194304 | tf_op jit(solution)/shard_map/all_to_all | solution.py:57
  84.4 1.4 %copy-start.1 = (f32[256,2048]{1,0:T(8,128)}, f32[256,2048]{1,0:T(8,128)S(1)}, u32[]{:S(2)}) copy-start(f32[256,2048]{1,0:T(8,128)S(1)} %fusion.11) | copy-start | bytes 6291460
  128.8 2.5 %copy-start.2 = (f32[256]{0:T(256)S(1)}, f32[256]{0:T(256)}, u32[]{:S(2)}) copy-start(f32[256]{0:T(256)} %param.9) | copy-start | bytes 3076
